TPU v7x, 32 devices: a whole 2x2x4 slice. The times are simulated.
32 devices in a mesh: graph: 8 (over z, x), mp: 4 (over y, core).
Axes of the slice: x: 2, y: 2, z: 4, core: 2. Of those that a mesh axis runs over, the one named last changes fastest.
Arguments:
- edge_state: bfloat16 [4096, 1536], P('graph', 'mp'), may hold values from -6 to 6
- down_weight: bfloat16 [1536, 384], P('mp'), may hold values from -0.15625 to 0.15625
- basis: float32 [42, 131072], P(None, ('graph', 'mp')), may hold values from -6 to 6
- basis_weight: float32 [42, 384], replicated, may hold values from -1 to 1
- up_weight: bfloat16 [384, 1536], P(None, 'mp'), may hold values from -0.3125 to 0.3125
- dense_weight: bfloat16 [3, 2, 1536, 1536], P(None, None, None, 'mp'), may hold values from -0.15625 to 0.15625
- send_rows: int32 [8, 32, 64], P('graph', 'mp'), may hold values from 0 to 512, as said below
- trip_in: int32 [131072], P(('graph', 'mp')), may hold values from 0 to 511, as said below
- trip_out: int32 [131072], P(('graph', 'mp')), may hold values from 0 to 511, as said below
- trip_live: int32 [131072], P(('graph', 'mp')), may hold values from 0 to 1, as said below
- edge_atom: int32 [4096], P('graph'), may hold values from 0 to 255
Outputs:
- edge_out: bfloat16 [4096, 1536], P('graph', 'mp')
- atom_out: bfloat16 [256, 1536], P('graph', 'mp')
Inputs may be any that keep to these rules, and one draw needn't show every extreme that they name: `send_rows`: entry [s, m * 8 + g, c] is a row among the 512 edges of graph index s listed in slot c for the device at graph index g and mp index m, or 512 for an empty slot; used slots come first in each list, and some device has every list full. `trip_in`: A slot s * 64 + c of the triplet's own device whose list entry from graph index s is used. `trip_out`: A slot s * 64 + c of the triplet's own device whose list entry from graph index s is used. `trip_live`: on each device the real triplets come first; some device has no padding.
All inputs are finite; a program needn't handle non-finite values.
Results may differ from a plain program's by a relative error of at most 0.014.
Values may be sent and summed in bfloat16 or wider, within the bound.
A program may use at most 128 MiB of HBM per device.

v0:
```python
import jax
import jax.numpy as jnp
from jax import lax
from jax.sharding import PartitionSpec as P

ATOM_DEV = 32


inv_root_two = 0.7071067811865476
atom_scale = 0.2


def dense_map(inputs, weight):
    return jnp.dot(
        lax.all_gather(inputs, "mp", axis=1, tiled=True), weight, preferred_element_type=jnp.float32
    )


def local(
    edge_state,
    down_weight,
    basis,
    basis_weight,
    up_weight,
    dense_weight,
    send_rows,
    trip_in,
    trip_out,
    trip_live,
    edge_atom,
):
    edge_rows = edge_state.shape[0]
    width = down_weight.shape[1]
    graph_size = lax.axis_size("graph")
    partial_value = jnp.dot(edge_state, down_weight, preferred_element_type=jnp.float32)
    projected = lax.psum(partial_value.astype(jnp.bfloat16), "mp")
    padded = jnp.concatenate([projected, jnp.zeros((1, width), jnp.bfloat16)], axis=0)
    row_lists = send_rows[0]
    outgoing = jnp.take(padded, row_lists, axis=0)
    received = lax.all_to_all(outgoing, "graph", split_axis=0, concat_axis=0, tiled=True)
    slot_total = received.shape[0] * received.shape[1]
    slot_rows = received.reshape(slot_total, width)
    angle_coef = lax.dot_general(
        basis,
        basis_weight,
        (((0,), (0,)), ((), ())),
        precision=lax.Precision.HIGHEST,
        preferred_element_type=jnp.float32,
    )
    trip_values = (
        jnp.take(slot_rows, trip_in, axis=0).astype(jnp.float32)
        * angle_coef
        * trip_live[:, None].astype(jnp.float32)
    )
    slot_sums = jax.ops.segment_sum(trip_values, trip_out, num_segments=slot_total).astype(
        jnp.bfloat16
    )
    returned = lax.all_to_all(
        slot_sums.reshape(received.shape), "graph", split_axis=0, concat_axis=0, tiled=True
    )
    edge_sums = jax.ops.segment_sum(
        returned.reshape(slot_total, width).astype(jnp.float32),
        row_lists.reshape(-1),
        num_segments=edge_rows + 1,
    )[:edge_rows]
    update_rows = lax.psum(edge_sums.astype(jnp.bfloat16), "mp")
    hidden = edge_state.astype(jnp.float32) + jnp.dot(
        update_rows, up_weight, preferred_element_type=jnp.float32
    )
    for layer_index in range(dense_weight.shape[0]):
        inner = jax.nn.silu(
            dense_map(hidden.astype(jnp.bfloat16), dense_weight[layer_index, 0])
        ).astype(jnp.bfloat16)
        outer = jax.nn.silu(dense_map(inner, dense_weight[layer_index, 1]))
        hidden = (hidden + outer) * inv_root_two
    atom_total = ATOM_DEV * graph_size
    partial_atoms = jax.ops.segment_sum(hidden, edge_atom, num_segments=atom_total)
    summed_atoms = lax.psum(partial_atoms, "graph")
    atom_table = jax.nn.silu(atom_scale * summed_atoms).astype(jnp.bfloat16)
    atom_out = lax.dynamic_slice_in_dim(atom_table, lax.axis_index("graph") * ATOM_DEV, ATOM_DEV, 0)
    edge_out = (hidden + jnp.take(atom_table, edge_atom, axis=0).astype(jnp.float32)).astype(
        jnp.bfloat16
    )
    return (edge_out, atom_out)


def solution(mesh):
    in_specs = (
        P("graph", "mp"),
        P("mp", None),
        P(None, ("graph", "mp")),
        P(),
        P(None, "mp"),
        P(None, None, None, "mp"),
        P("graph", "mp", None),
        P(("graph", "mp")),
        P(("graph", "mp")),
        P(("graph", "mp")),
        P("graph"),
    )
    out_specs = (P("graph", "mp"), P("graph", "mp"))
    return jax.shard_map(local, mesh=mesh, in_specs=in_specs, out_specs=out_specs, check_vma=False)
```

profile of v0, /device:TPU:0, one launch (start us, length us, event | category | flops | bytes accessed | tf_op | source)
XLA Modules:
  0.0 392.1 jit_solution(13669747113387976459)
XLA Ops:
  7.2 2.3 convolution_convert_fusion
  11.0 35.5 %all-reduce.5.cloned.1.call-done = bf16[512,384]{1,0:T(8,128)(2,1)} async-done(((bf16[512,384]{1,0:T(8,128)(2,1)}), bf16[512,384]{1,0:T(8,128)(2,1)}) %all-reduce.5.cloned.1.call-update) | async-done | bytes 393232 | tf_op jit(solution)/shard_map/psum | solution.py:36
  50.4 5.5 %all-to-all-start = ((bf16[8,64,384]{2,1,0:T(8,128)(2,1)}), bf16[8,64,384]{2,1,0:T(8,128)(2,1)S(1)}, u32[]{:S(2)}, u32[]{:S(2)}) async-start(bf16[8,64,384]{2,1,0:T(8,128)(2,1)} %broadcast_select_fusion), calls=%async_computation | async-start | bytes 786432 | tf_op jit(solution)/shard_map/all_to_all | solution.py:40
  56.0 7.1 %fusion.49 = f32[4096,384]{1,0:T(8,128)} fusion(f32[42,4096]{1,0:T(8,128)S(1)} %copy-done, f32[42,384]{1,0:T(8,128)S(1)} %copy-done.3), kind=kOutput, calls=%fused_computation.65 | convolution fusion | flops 792723456 | bytes 7044096 | tf_op jit(solution)/shard_map/dot_general | solution.py:43
  63.1 3.4 all-to-all-done
  66.5 44.3 %scatter_custom_fusion = f32[512,384]{1,0:T(8,128)S(1)} fusion(s32[4096]{0:T(1024)} %param.19, f32[4096,384]{1,0:T(8,128)} %fusion.49, f32[4096]{0:T(1024)S(1)} %convert_element_type.53, pred[4096]{0:T(1024)(128)(4,1)S(1)} %compare_and_fusion, bf16[]{:T(256)} %constant.64.clone.1, f32[]{:T(128)} %constant.41.clone.1, bf16[512,384]{1,0:T(8,128)(2,1)S(1)} %bitcast.59, ...), kind=kCustom, calls=%fused_computation.6 | custom fusion | flops 7864320 | bytes 7508992 | tf_op jit(solution)/shard_map/scatter-add | solution.py:55
  111.6 3.8 all-to-all-start.1
  115.7 10.7 %all-to-all-done.1 = bf16[8,64,384]{2,1,0:T(8,128)(2,1)S(1)} async-done(((bf16[8,64,384]{2,1,0:T(8,128)(2,1)}), bf16[8,64,384]{2,1,0:T(8,128)(2,1)S(1)}, u32[]{:S(2)}, u32[]{:S(2)}) %all-to-all-start.1) | async-done | bytes 393248 | tf_op jit(solution)/shard_map/all_to_all | solution.py:58
  126.5 3.9 scatter_custom_fusion.1
  131.2 32.1 %all-reduce.7.cloned.1.call-done = bf16[512,384]{1,0:T(8,128)(2,1)} async-done(((bf16[512,384]{1,0:T(8,128)(2,1)}), bf16[512,384]{1,0:T(8,128)(2,1)}) %all-reduce.7.cloned.1.call-update) | async-done | bytes 393232 | tf_op jit(solution)/shard_map/psum | solution.py:66
  165.5 19.7 %all-gather.7.cloned.1.call-done = bf16[512,1536]{1,0:T(8,128)(2,1)} async-done(((bf16[512,384]{1,0:T(8,128)(2,1)}), bf16[512,1536]{1,0:T(8,128)(2,1)}) %all-gather.7.cloned.1.call-update) | async-done | bytes 1572880 | tf_op jit(solution)/shard_map/all_gather | solution.py:15
  185.2 3.5 multiply_convert_fusion.2
  188.8 19.7 %all-gather.9.cloned.1.call-done = bf16[512,1536]{1,0:T(8,128)(2,1)} async-done(((bf16[512,384]{1,0:T(8,128)(2,1)}), bf16[512,1536]{1,0:T(8,128)(2,1)}) %all-gather.9.cloned.1.call-update) | async-done | bytes 1572880 | tf_op jit(solution)/shard_map/all_gather | solution.py:15
  208.5 3.6 fusion.47
  212.2 19.7 %all-gather.11.cloned.1.call-done = bf16[512,1536]{1,0:T(8,128)(2,1)} async-done(((bf16[512,384]{1,0:T(8,128)(2,1)}), bf16[512,1536]{1,0:T(8,128)(2,1)}) %all-gather.11.cloned.1.call-update) | async-done | bytes 1572880 | tf_op jit(solution)/shard_map/all_gather | solution.py:15
  231.9 3.5 multiply_convert_fusion.1
  235.5 19.7 %all-gather.13.cloned.1.call-done = bf16[512,1536]{1,0:T(8,128)(2,1)} async-done(((bf16[512,384]{1,0:T(8,128)(2,1)}), bf16[512,1536]{1,0:T(8,128)(2,1)}) %all-gather.13.cloned.1.call-update) | async-done | bytes 1572880 | tf_op jit(solution)/shard_map/all_gather | solution.py:15
  255.2 3.6 fusion.48
  258.9 19.7 %all-gather.15.cloned.1.call-done = bf16[512,1536]{1,0:T(8,128)(2,1)} async-done(((bf16[512,384]{1,0:T(8,128)(2,1)}), bf16[512,1536]{1,0:T(8,128)(2,1)}) %all-gather.15.cloned.1.call-update) | async-done | bytes 1572880 | tf_op jit(solution)/shard_map/all_gather | solution.py:15
  278.6 3.5 multiply_convert_fusion
  282.2 19.7 %all-gather.17.cloned.1.call-done = bf16[512,1536]{1,0:T(8,128)(2,1)} async-done(((bf16[512,384]{1,0:T(8,128)(2,1)}), bf16[512,1536]{1,0:T(8,128)(2,1)}) %all-gather.17.cloned.1.call-update) | async-done | bytes 1572880 | tf_op jit(solution)/shard_map/all_gather | solution.py:15
  301.9 2.8 add_multiply_fusion
  304.8 4.3 %scatter_custom_fusion.2 = f32[256,384]{1,0:T(8,128)} fusion(s32[512]{0:T(512)S(1)} %copy-done.7, f32[512,384]{1,0:T(8,128)S(1)} %add_multiply_fusion, f32[]{:T(128)} %constant.41.clone.1), kind=kCustom, calls=%fused_computation.48 | custom fusion | flops 196608 | bytes 393220 | tf_op jit(solution)/shard_map/scatter-add | solution.py:77
  309.1 71.9 %all-reduce.9.cloned.1.call-done = f32[256,384]{1,0:T(8,128)} async-done(((f32[256,384]{1,0:T(8,128)}), f32[256,384]{1,0:T(8,128)}) %all-reduce.9.cloned.1.call-update) | async-done | bytes 393232 | tf_op jit(solution)/shard_map/psum | solution.py:78
  (55 shorter events, 14.5 us)
Async XLA Ops:
  7.2 48.8 %copy-start = (f32[42,4096]{1,0:T(8,128)S(1)}, f32[42,4096]{1,0:T(8,128)}, u32[]{:S(2)}) copy-start(f32[42,4096]{1,0:T(8,128)} %param.13) | copy-start | bytes 2064388
  7.2 39.3 %all-reduce.5.cloned.1.call-start = ((), (), s32[]{:S(2)}) async-start(), calls=%async_computation.2 | async-start | bytes 786432 | tf_op jit(solution)/shard_map/psum | solution.py:36
  49.5 6.4 %copy-start.4 = (s32[4096]{0:T(1024)S(1)}, s32[4096]{0:T(1024)}, u32[]{:S(2)}) copy-start(s32[4096]{0:T(1024)} %param.18) | copy-start | bytes 49156
  49.5 6.5 %copy-start.6 = (s32[4096]{0:T(1024)S(1)}, s32[4096]{0:T(1024)}, u32[]{:S(2)}) copy-start(s32[4096]{0:T(1024)} %param.20) | copy-start | bytes 49156
  49.5 6.5 %copy-start.3 = (f32[42,384]{1,0:T(8,128)S(1)}, f32[42,384]{1,0:T(8,128)}, u32[]{:S(2)}) copy-start(f32[42,384]{1,0:T(8,128)} %param.14) | copy-start | bytes 193540
  50.4 16.1 %all-to-all-start = ((bf16[8,64,384]{2,1,0:T(8,128)(2,1)}), bf16[8,64,384]{2,1,0:T(8,128)(2,1)S(1)}, u32[]{:S(2)}, u32[]{:S(2)}) async-start(bf16[8,64,384]{2,1,0:T(8,128)(2,1)} %broadcast_select_fusion), calls=%async_computation | async-start | bytes 786432 | tf_op jit(solution)/shard_map/all_to_all | solution.py:40
  110.8 4.8 %copy-start.5 = (s32[1,8,64]{2,1,0:T(8,128)S(1)}, s32[1,8,64]{2,1,0:T(8,128)}, u32[]{:S(2)}) copy-start(s32[1,8,64]{2,1,0:T(8,128)} %param.17) | copy-start | bytes 6148
  111.6 51.7 %copy-start.1 = (bf16[512,384]{1,0:T(8,128)(2,1)S(1)}, bf16[512,384]{1,0:T(8,128)(2,1)}, u32[]{:S(2)}) copy-start(bf16[512,384]{1,0:T(8,128)(2,1)} %param.11) | copy-start | bytes 1179652
  111.6 51.7 %copy-start.2 = (bf16[384,384]{1,0:T(8,128)(2,1)S(1)}, bf16[384,384]{1,0:T(8,128)(2,1)}, u32[]{:S(2)}) copy-start(bf16[384,384]{1,0:T(8,128)(2,1)} %param.15) | copy-start | bytes 884740
  111.6 14.9 %all-to-all-start.1 = ((bf16[8,64,384]{2,1,0:T(8,128)(2,1)}), bf16[8,64,384]{2,1,0:T(8,128)(2,1)S(1)}, u32[]{:S(2)}, u32[]{:S(2)}) async-start(bf16[8,64,384]{2,1,0:T(8,128)(2,1)} %bitcast.4), calls=%async_computation.1 | async-start | bytes 786432 | tf_op jit(solution)/shard_map/all_to_all | solution.py:58
  115.4 47.8 %all-reduce.7.cloned.1.call-start = ((), (), s32[]{:S(2)}) async-start(), calls=%async_computation.3 | async-start | bytes 786432 | tf_op jit(solution)/shard_map/psum | solution.py:66
  131.2 54.0 %all-gather.7.cloned.1.call-start = ((), (), s32[]{:S(2)}) async-start(), calls=%async_computation.4 | async-start | bytes 1966080 | tf_op jit(solution)/shard_map/all_gather | solution.py:15
  165.4 43.1 %all-gather.9.cloned.1.call-start = ((), (), s32[]{:S(2)}) async-start(), calls=%async_computation.5 | async-start | bytes 1966080 | tf_op jit(solution)/shard_map/all_gather | solution.py:15
  188.8 43.1 %all-gather.11.cloned.1.call-start = ((), (), s32[]{:S(2)}) async-start(), calls=%async_computation.6 | async-start | bytes 1966080 | tf_op jit(solution)/shard_map/all_gather | solution.py:15
  212.1 43.1 %all-gather.13.cloned.1.call-start = ((), (), s32[]{:S(2)}) async-start(), calls=%async_computation.7 | async-start | bytes 1966080 | tf_op jit(solution)/shard_map/all_gather | solution.py:15
  235.5 43.1 %all-gather.15.cloned.1.call-start = ((), (), s32[]{:S(2)}) async-start(), calls=%async_computation.8 | async-start | bytes 1966080 | tf_op jit(solution)/shard_map/all_gather | solution.py:15
  258.8 43.1 %all-gather.17.cloned.1.call-start = ((), (), s32[]{:S(2)}) async-start(), calls=%async_computation.9 | async-start | bytes 1966080 | tf_op jit(solution)/shard_map/all_gather | solution.py:15
  282.2 98.8 %all-reduce.9.cloned.1.call-start = ((), (), s32[]{:S(2)}) async-start(), calls=%async_computation.10 | async-start | bytes 786432 | tf_op jit(solution)/shard_map/psum | solution.py:78
  301.9 2.8 copy-start.7
Sparse Core Ops, SparseCore 0:
  10.9 35.5 all-reduce.4
  131.3 31.9 all-reduce.6
  165.6 19.5 all-gather.6
  188.9 19.6 all-gather.8
  212.2 19.6 all-gather.10
  235.6 19.6 all-gather.12
  258.9 19.6 all-gather.14
  282.3 19.6 all-gather.16
  309.2 71.7 all-reduce.8
where the time goes:
time: 393 us; the launch traced here: 392 us
  waiting for transfers between devices  272 us (69%)
  other arithmetic  57.6 us (15%)
  matrix products  32.1 us (8%)
  between operations  14 us (4%)
  starting transfers between devices  9.87 us (3%)
  local copies, waits for them, and re-layouts  6.52 us (2%)
    all_gather x6, waiting for transfers between devices, dense_map(): lax.all_gather(inputs, 'mp', axis=1, tiled=True)  118 us
    psum x1, waiting for transfers between devices, local(): summed_atoms = lax.psum(partial_atoms, 'graph')  71.9 us
    scatter-add x1, other arithmetic, local(): jax.ops.segment_sum(trip_values, trip_out, num_segments=slot_total)  44.3 us
    psum x1, waiting for transfers between devices, local(): projected = lax.psum(partial_value.astype(jnp.bfloat16), 'mp')  35.5 us
    psum x1, waiting for transfers between devices, local(): update_rows = lax.psum(edge_sums.astype(jnp.bfloat16), 'mp')  32.1 us
    dot_general x6, matrix products, dense_map(): jnp.dot(lax.all_gather(inputs, 'mp', axis=1, tiled=True), weight, preferr...  20.6 us
    all_to_all x1, waiting for transfers between devices, local(): lax.all_to_all(slot_sums.reshape(received.shape), 'graph', split_axis=0,...  10.7 us
  transfers between devices with their start and end apart: 11, of which 11 were waited for; matrix products, arithmetic and copies ran while one was open for 2% of the time, Pallas kernels for 0%

commit v1 on v0

v1 whole, which is shorter than its diff:
```python
import functools

import jax
import jax.numpy as jnp
from jax import lax
from jax.experimental import pallas as pl
from jax.experimental.pallas import tpu as pltpu
from jax.sharding import PartitionSpec as P

ATOM_DEV = 32
CHUNKS = 4

inv_root_two = 0.7071067811865476
atom_scale = 0.2

MESH = pl.DeviceIdType.MESH
bf16 = jnp.bfloat16
f32 = jnp.float32


def silu(v):
    return v / (1.0 + jnp.exp(-v))


def flip(index, bit):
    return index + bit - 2 * bit * ((index // bit) % 2)


def one_hot(rows, ids):
    shape = (rows, ids.shape[1])
    return jnp.where(lax.broadcasted_iota(jnp.int32, shape, 0) == ids, 1.0, 0.0).astype(bf16)


def dot(a, b, ca=1, cb=0):
    return lax.dot_general(a, b, (((ca,), (cb,)), ((), ())), preferred_element_type=f32)


def gather_plan(mp):
    plan, held, bit = [], [0], mp // 2
    while bit >= 1:
        plan += [(bit, off) for off in held]
        held += [bit ^ off for off in held]
        bit //= 2
    return plan, held


def kernel(
    graph, mp, tile,
    state_ref, down_ref, basis_ref, bw_ref, up_ref, dense_hbm, lists_ref, in_ref, out_ref, live_ref, atom_ref,
    edge_out_ref, atom_out_ref,
    weight, weight_sem,
    part_a, got_a, sum_a, more_a, full_a,
    part_b, got_b, sum_b, more_b, full_b,
    red_send, red_recv,
    to_a, from_a, to_b, from_b, xc_send, xc_recv,
    recv_t, angle, slots,
    acts, hidden, act_send, act_recv,
    atoms_own, atoms_to, atoms_from, table,
    bar_dummy,
):
    g = lax.axis_index("graph")
    m = lax.axis_index("mp")
    rows, width = state_ref.shape
    trip = down_ref.shape[1]
    layers = weight.shape[0] // 2
    slot_total = slots.shape[0]
    cap = slot_total // graph
    triplets = in_ref.shape[1]
    atoms = graph * ATOM_DEV
    half = rows // 2
    bits = [1 << i for i in range(mp.bit_length() - 1)]

    load = pltpu.make_async_copy(dense_hbm, weight, weight_sem)
    load.start()

    barrier = pltpu.get_barrier_semaphore()

    def greet(k, _):
        pl.semaphore_signal(barrier, inc=1, device_id={"graph": (g + k) % graph}, device_id_type=MESH)
        return 0

    lax.fori_loop(1, graph, greet, 0)
    for bit in bits:
        pl.semaphore_signal(barrier, inc=1, device_id={"mp": flip(m, bit)}, device_id_type=MESH)

    def mp_copy(src, dst, which, slot, bit):
        return pltpu.make_async_remote_copy(
            src_ref=src, dst_ref=dst, send_sem=red_send.at[which, slot], recv_sem=red_recv.at[which, slot],
            device_id={"mp": flip(m, bit)}, device_id_type=MESH)

    mine = pl.multiple_of((m % 2) * half, half)
    other = pl.multiple_of(half - (m % 2) * half, half)

    def mp_sum(which, part, got, summed, more, full):
        first = mp_copy(part.at[pl.ds(other, half)], got, which, 0, 1)
        first.start()
        first.wait()
        total = part[pl.ds(mine, half)].astype(f32) + got[...].astype(f32)
        for i, bit in enumerate(bits[1:]):
            summed[i] = total.astype(bf16)
            step = mp_copy(summed.at[i], more.at[i], which, 1 + i, bit)
            step.start()
            step.wait()
            total = summed[i].astype(f32) + more[i].astype(f32)
        full[pl.ds(mine, half)] = total.astype(bf16)
        last = mp_copy(full.at[pl.ds(mine, half)], full.at[pl.ds(mine, half)], which, len(bits), 1)
        last.start()
        last.wait()

    def exchange(which, src_at, dst, dst_at, size):
        def copy(k):
            peer = (g + k) % graph
            return pltpu.make_async_remote_copy(
                src_ref=src_at(peer), dst_ref=dst_at(g),
                send_sem=xc_send.at[which, k], recv_sem=xc_recv.at[which, k],
                device_id={"graph": peer}, device_id_type=MESH)

        def start(k, _):
            copy(k).start()
            return 0

        def wait(k, _):
            copy(k).wait()
            return 0

        return (lambda: lax.fori_loop(1, graph, start, 0)), (lambda: lax.fori_loop(1, graph, wait, 0))

    def block(ref, size):
        return lambda i: ref.at[pl.ds(pl.multiple_of(i * size, size), size)]

    part_a[...] = dot(state_ref[...], down_ref[...]).astype(bf16)
    pl.semaphore_wait(barrier, graph - 1 + len(bits))
    mp_sum(0, part_a, got_a, sum_a, more_a, full_a)

    step_rows = min(slot_total, 512)
    own = pl.ds(pl.multiple_of(g * cap, cap), cap)

    def pick(i, _):
        at = pl.ds(pl.multiple_of(i * step_rows, step_rows), step_rows)
        lists = one_hot(rows, lists_ref[:, at])
        to_a[at, :] = dot(lists, full_a[...], 0, 0).astype(bf16)
        return 0

    lax.fori_loop(0, slot_total // step_rows, pick, 0)
    start, wait = exchange(0, block(to_a, cap), from_a, block(from_a, cap), cap)
    start()
    from_a[own] = to_a[own]

    def angles(i, _):
        at = pl.ds(pl.multiple_of(i * tile, tile), tile)
        angle[:, at] = lax.dot_general(
            bw_ref[...], basis_ref[:, at], (((1,), (0,)), ((), ())),
            precision=lax.Precision.HIGHEST, preferred_element_type=f32)
        return 0

    lax.fori_loop(0, triplets // tile, angles, 0)
    slots[...] = jnp.zeros_like(slots)
    wait()

    recv_t[...] = from_a[...].astype(f32).T.astype(bf16)

    def trips(i, _):
        at = pl.ds(pl.multiple_of(i * tile, tile), tile)
        source = one_hot(slot_total, in_ref[:, at])
        value = dot(recv_t[...], source) * angle[:, at]
        target = one_hot(slot_total, jnp.where(live_ref[:, at] > 0, out_ref[:, at], -1))
        slots[...] += dot(target, value.astype(bf16), 1, 1)
        return 0

    lax.fori_loop(0, triplets // tile, trips, 0)
    to_b[...] = slots[...].astype(bf16)

    start, wait = exchange(1, block(to_b, cap), from_b, block(from_b, cap), cap)
    start()
    from_b[own] = to_b[own]
    wait()

    def put(i, total):
        at = pl.ds(pl.multiple_of(i * step_rows, step_rows), step_rows)
        return total + dot(one_hot(rows, lists_ref[:, at]), from_b[at, :])

    if slot_total == step_rows:
        part_b[...] = dot(one_hot(rows, lists_ref[...]), from_b[...]).astype(bf16)
    else:
        hidden[:, :trip] = jnp.zeros((rows, trip), f32)

        def put(i, _):
            at = pl.ds(pl.multiple_of(i * step_rows, step_rows), step_rows)
            hidden[:, :trip] += dot(one_hot(rows, lists_ref[:, at]), from_b[at, :])
            return 0

        lax.fori_loop(0, slot_total // step_rows, put, 0)
        part_b[...] = hidden[:, :trip].astype(bf16)
    mp_sum(1, part_b, got_b, sum_b, more_b, full_b)

    plan, held = gather_plan(mp)
    size = rows // CHUNKS

    def other_of(off):
        index = m
        for bit in bits:
            if off & bit:
                index = flip(index, bit)
        return index

    def act_copy(layer, c, which):
        bit, off = plan[which]
        at = acts.at[layer, other_of(off), pl.ds(c * size, size)]
        return pltpu.make_async_remote_copy(
            src_ref=at, dst_ref=at,
            send_sem=act_send.at[layer, c, which], recv_sem=act_recv.at[layer, c, which],
            device_id={"mp": flip(m, bit)}, device_id_type=MESH)

    local = [i for i, (bit, off) in enumerate(plan) if off == 0]
    relayed = [i for i, (bit, off) in enumerate(plan) if off != 0]
    brings = {bit ^ off: i for i, (bit, off) in enumerate(plan)}
    relays_from = sorted({brings[plan[i][1]] for i in relayed})

    def send(layer, c):
        for i in local:
            act_copy(layer, c, i).start()

    def relay(layer, c):
        for i in relayed:
            first = brings[plan[i][1]]
            if [j for j in relayed if brings[plan[j][1]] == first][0] == i:
                act_copy(layer, c, first).wait_recv()
            act_copy(layer, c, i).start()

    def finish(layer, c):
        for i in range(len(plan)):
            if i not in relays_from:
                act_copy(layer, c, i).wait_recv()

    for c in range(CHUNKS):
        at = pl.ds(c * size, size)
        first = state_ref[at, :].astype(f32) + dot(full_b[at, :], up_ref[...])
        hidden[at, :] = first
        acts[0, m, at, :] = first.astype(bf16)
        send(0, c)

    load.wait()
    relay(0, 0)

    def layer_step(l, _):
        for inside in range(2):
            k = 2 * l + inside
            for c in range(CHUNKS):
                at = pl.ds(c * size, size)
                if c + 1 < CHUNKS:
                    relay(k, c + 1)
                elif inside == 0:
                    relay(k + 1, 0)
                else:
                    @pl.when(l + 1 < layers)
                    def _():
                        relay(k + 1, 0)
                finish(k, c)
                total = None
                for off in held:
                    index = other_of(off)
                    term = dot(acts[k, index, at, :], weight[k, pl.ds(pl.multiple_of(index * width, width), width), :])
                    total = term if total is None else total + term
                value = silu(total)
                if inside == 0:
                    acts[k + 1, m, at, :] = value.astype(bf16)
                    send(k + 1, c)
                else:
                    value = (hidden[at, :] + value) * inv_root_two
                    hidden[at, :] = value

                    @pl.when(l + 1 < layers)
                    def _():
                        acts[k + 1, m, at, :] = value.astype(bf16)
                        send(k + 1, c)
        return 0

    lax.fori_loop(0, layers, layer_step, 0)

    atom_rows = min(atoms, 256)

    def collect(i, _):
        at = pl.ds(pl.multiple_of(i * atom_rows, atom_rows), atom_rows)
        ids = one_hot(atom_rows, atom_ref[...] - i * atom_rows)
        high = hidden[...].astype(bf16)
        low = (hidden[...] - high.astype(f32)).astype(bf16)
        total = dot(ids, high) + dot(ids, low)
        atoms_own[at, :] = total
        atoms_to[at, :] = total.astype(bf16)
        return 0

    lax.fori_loop(0, atoms // atom_rows, collect, 0)
    start, wait = exchange(2, block(atoms_to, ATOM_DEV), atoms_from, block(atoms_from, ATOM_DEV), ATOM_DEV)
    start()
    here = pl.ds(pl.multiple_of(g * ATOM_DEV, ATOM_DEV), ATOM_DEV)
    atoms_from[here] = jnp.zeros((ATOM_DEV, width), bf16)
    wait()

    def add(i, total):
        return total + atoms_from[pl.ds(pl.multiple_of(i * ATOM_DEV, ATOM_DEV), ATOM_DEV)].astype(f32)

    total = lax.fori_loop(0, graph, add, atoms_own[here])
    mine_out = silu(atom_scale * total).astype(bf16)
    table[here] = mine_out
    atom_out_ref[...] = mine_out
    start, wait = exchange(3, lambda peer: block(table, ATOM_DEV)(g), table, block(table, ATOM_DEV), ATOM_DEV)
    start()

    def drain(k, _):
        for c in range(CHUNKS):
            for i in range(len(plan)):
                act_copy(k, c, i).wait_send()
        return 0

    lax.fori_loop(0, 2 * layers, drain, 0)
    wait()

    def spread(i, _):
        at = pl.ds(pl.multiple_of(i * atom_rows, atom_rows), atom_rows)
        hidden[...] += dot(one_hot(atom_rows, atom_ref[...] - i * atom_rows), table[at, :], 0, 0)
        return 0

    lax.fori_loop(0, atoms // atom_rows, spread, 0)
    edge_out_ref[...] = hidden[...].astype(bf16)


def local(graph, mp, edge_state, down_weight, basis, basis_weight, up_weight, dense_weight,
          send_rows, trip_in, trip_out, trip_live, edge_atom):
    rows, width = edge_state.shape
    trip = down_weight.shape[1]
    slot_total = graph * send_rows.shape[2]
    triplets = trip_in.shape[0]
    maps = dense_weight.shape[0] * dense_weight.shape[1]
    tile = 512 if slot_total <= 512 else 128
    atoms = graph * ATOM_DEV
    stages = mp.bit_length()
    extra = max(stages - 2, 1)
    half = rows // 2
    vmem = pltpu.VMEM
    reduce_bufs = [
        vmem((rows, trip), bf16), vmem((half, trip), bf16), vmem((extra, half, trip), bf16),
        vmem((extra, half, trip), bf16), vmem((rows, trip), bf16),
    ]
    dma = pltpu.SemaphoreType.DMA
    spec = pl.BlockSpec(memory_space=pltpu.VMEM)
    return pl.pallas_call(
        functools.partial(kernel, graph, mp, tile),
        out_shape=(
            jax.ShapeDtypeStruct((rows, width), bf16),
            jax.ShapeDtypeStruct((ATOM_DEV, width), bf16),
        ),
        in_specs=[spec] * 5 + [pl.BlockSpec(memory_space=pl.ANY)] + [spec] * 5,
        out_specs=(spec, spec),
        scratch_shapes=[
            vmem((maps,) + dense_weight.shape[2:], bf16), dma(()),
            *reduce_bufs, *reduce_bufs,
            dma((2, stages)), dma((2, stages)),
            vmem((slot_total, trip), bf16), vmem((slot_total, trip), bf16),
            vmem((slot_total, trip), bf16), vmem((slot_total, trip), bf16),
            dma((4, graph)), dma((4, graph)),
            vmem((trip, slot_total), bf16), vmem((trip, triplets), f32), vmem((slot_total, trip), f32),
            vmem((maps, mp, rows, width), bf16), vmem((rows, max(width, trip)), f32),
            dma((maps, CHUNKS, mp - 1)), dma((maps, CHUNKS, mp - 1)),
            vmem((atoms, width), f32), vmem((atoms, width), bf16), vmem((atoms, width), bf16),
            vmem((atoms, width), bf16),
            vmem((8, 128), f32),
        ],
        compiler_params=pltpu.CompilerParams(
            collective_id=0, has_side_effects=True, vmem_limit_bytes=64000 * 1024
        ),
        name="edge_block",
    )(
        edge_state, down_weight, basis, basis_weight.T, up_weight,
        dense_weight.reshape((maps,) + dense_weight.shape[2:]),
        send_rows.reshape(1, slot_total), trip_in.reshape(1, triplets), trip_out.reshape(1, triplets),
        trip_live.reshape(1, triplets), edge_atom.reshape(1, rows),
    )


def solution(mesh):
    in_specs = (
        P("graph", "mp"),
        P("mp", None),
        P(None, ("graph", "mp")),
        P(),
        P(None, "mp"),
        P(None, None, None, "mp"),
        P("graph", "mp", None),
        P(("graph", "mp")),
        P(("graph", "mp")),
        P(("graph", "mp")),
        P("graph"),
    )
    out_specs = (P("graph", "mp"), P("graph", "mp"))
    body = functools.partial(local, mesh.shape["graph"], mesh.shape["mp"])
    return jax.shard_map(body, mesh=mesh, in_specs=in_specs, out_specs=out_specs, check_vma=False)
```

time: 393 us -> 130 us (0.33)
  waiting for transfers between devices: 272 us -> 0 us
  Pallas kernels: 0 us -> 123 us
  other arithmetic: 57.6 us -> 0 us
  matrix products: 32.1 us -> 0 us
  between operations: 14 us -> 0.64 us
  starting transfers between devices: 9.87 us -> 0 us
    psum x3 -> x0, waiting for transfers between devices: 139 us -> none  [the longest x1 71.9 us: local(): summed_atoms = lax.psum(partial_atoms, 'graph')]
    pallas_call x0 -> x1, Pallas kernels: none -> 123 us  [local(): pl.pallas_call(functools.partial(kernel, graph, mp, tile), out_shape=(jax...]
    all_gather x6 -> x0, waiting for transfers between devices: 118 us -> none  [dense_map(): lax.all_gather(inputs, 'mp', axis=1, tiled=True)]
    scatter-add x3 -> x0, other arithmetic: 52.5 us -> none  [the longest x1 44.3 us: local(): jax.ops.segment_sum(trip_values, trip_out, num_segments=slot_total)]
    dot_general x9 -> x0, matrix products: 32.1 us -> none  [the longest x6 20.6 us: dense_map(): jnp.dot(lax.all_gather(inputs, 'mp', axis=1, tiled=True), weight, preferr...]
    all_to_all x2 -> x0, waiting for transfers between devices: 14.1 us -> none  [the longest x1 10.7 us: local(): lax.all_to_all(slot_sums.reshape(received.shape), 'graph', split_axis=0,...]
    all_to_all x2 -> x0, starting transfers between devices: 9.32 us -> none  [the longest x1 5.51 us: local(): lax.all_to_all(outgoing, 'graph', split_axis=0, concat_axis=0, tiled=True)]
    unnamed x16 -> x3, local copies, waits for them, and re-layouts: 0.05 us -> 4.82 us
  transfers between devices with their start and end apart: 11 -> 0, of which waited for: 11 -> 0; matrix products, arithmetic and copies ran while one was open for 2% -> 0% of each run, Pallas kernels for 0% -> 0%
where the time goes in v1:
time: 130 us
  Pallas kernels  123 us (95%)
  local copies, waits for them, and re-layouts  6.16 us (5%)
    pallas_call x1, Pallas kernels, local(): pl.pallas_call(functools.partial(kernel, graph, mp, tile), out_shape=(jax...  123 us
    unnamed x3, local copies, waits for them, and re-layouts  4.82 us

profile of v1, /device:TPU:0, one launch (start us, length us, event | category | flops | bytes accessed | tf_op | source)
XLA Modules:
  0.0 129.9 jit_solution(17209475183001970296)
XLA Ops:
  0.6 1.3 %reshape.23.lists_ref = s32[1,512]{1,0:T(1,128)} reshape(s32[1,8,64]{2,1,0:T(8,128)} %param.17) | data formatting | bytes 4096 | tf_op jit(solution)/shard_map/reshape | solution.py:375
  2.0 1.7 %copy.13 = f32[42,384]{0,1:T(8,128)} copy(f32[42,384]{1,0:T(8,128)} %param.14) | data formatting | bytes 129024 | tf_op args[3]
  3.7 123.1 %edge_block.1 = (bf16[512,384]{1,0:T(8,128)(2,1)}, bf16[32,384]{1,0:T(8,128)(2,1)}) custom-call(bf16[512,384]{1,0:T(8,128)(2,1)} %state_ref.1, bf16[384,384]{1,0:T(8,128)(2,1)} %down_ref.1, f32[42,4096]{1,0:T(8,128)} %basis_ref.1, f32[384,42]{1,0:T(8,128)} %bitcast.7, bf16[384,384]{1,0:T(8,128)(2,1)} %up_ref.1, bf16[6,1536,384]{2,1,0:T(8,128)(2,1)} %bitcast.6, ...), custom_call_target="tpu_custom_call" | custom-call | tf_op jit(solution)/shard_map/edge_block/pallas_call | solution.py:346
  126.8 1.8 %copy.16 = bf16[512,384]{1,0:T(8,128)(2,1)} copy(bf16[512,384]{1,0:T(8,128)(2,1)} %get-tuple-element.4) | data formatting | bytes 786432
  128.6 1.3 %copy.17 = bf16[32,384]{1,0:T(8,128)(2,1)} copy(bf16[32,384]{1,0:T(8,128)(2,1)} %get-tuple-element.5) | data formatting | bytes 49152

commit v2 on v1

--- a/solution.py
+++ b/solution.py
@@ -53,18 +53,19 @@
     part_b, got_b, sum_b, more_b, full_b,
     red_send, red_recv,
     to_a, from_a, to_b, from_b, xc_send, xc_recv,
-    recv_t, angle, slots,
+    lists_flat, list_hot, angle, slots, in_hot, out_hot,
     acts, hidden, act_send, act_recv,
     atoms_own, atoms_to, atoms_from, table,
-    bar_dummy,
 ):
     g = lax.axis_index("graph")
     m = lax.axis_index("mp")
     rows, width = state_ref.shape
     trip = down_ref.shape[1]
     layers = weight.shape[0] // 2
-    slot_total = slots.shape[0]
-    cap = slot_total // graph
+    cap = lists_ref.shape[2]
+    slot_total = graph * cap
+    pieces, lane = to_a.shape[0], to_a.shape[2]
+    kept = in_hot is not None
     triplets = in_ref.shape[1]
     atoms = graph * ATOM_DEV
     half = rows // 2
@@ -83,29 +84,49 @@
     for bit in bits:
         pl.semaphore_signal(barrier, inc=1, device_id={"mp": flip(m, bit)}, device_id_type=MESH)
 
-    def mp_copy(src, dst, which, slot, bit):
+    def mp_copy(src, dst, which, slot, i, bit):
         return pltpu.make_async_remote_copy(
-            src_ref=src, dst_ref=dst, send_sem=red_send.at[which, slot], recv_sem=red_recv.at[which, slot],
+            src_ref=src, dst_ref=dst, send_sem=red_send.at[which, slot, i], recv_sem=red_recv.at[which, slot, i],
             device_id={"mp": flip(m, bit)}, device_id_type=MESH)
 
     mine = pl.multiple_of((m % 2) * half, half)
     other = pl.multiple_of(half - (m % 2) * half, half)
-
-    def mp_sum(which, part, got, summed, more, full):
-        first = mp_copy(part.at[pl.ds(other, half)], got, which, 0, 1)
-        first.start()
-        first.wait()
-        total = part[pl.ds(mine, half)].astype(f32) + got[...].astype(f32)
-        for i, bit in enumerate(bits[1:]):
-            summed[i] = total.astype(bf16)
-            step = mp_copy(summed.at[i], more.at[i], which, 1 + i, bit)
-            step.start()
-            step.wait()
-            total = summed[i].astype(f32) + more[i].astype(f32)
-        full[pl.ds(mine, half)] = total.astype(bf16)
-        last = mp_copy(full.at[pl.ds(mine, half)], full.at[pl.ds(mine, half)], which, len(bits), 1)
-        last.start()
-        last.wait()
+    size = rows // CHUNKS
+    subs = range(CHUNKS // 2)
+
+    def mp_sum(which, part, got, summed, more, full, meanwhile=None, ready=None):
+        at = [pl.ds(i * size, size) for i in subs]
+        firsts = [mp_copy(part.at[pl.ds(other + i * size, size)], got.at[at[i]], which, 0, i, 1) for i in subs]
+        steps = [[mp_copy(summed.at[b, at[i]], more.at[b, at[i]], which, 1 + b, i, bit) for i in subs]
+                 for b, bit in enumerate(bits[1:])]
+        for first in firsts:
+            first.start()
+
+        def total(b, i):
+            if b == 0:
+                return part[pl.ds(mine + i * size, size)].astype(f32) + got[at[i]].astype(f32)
+            return summed[b - 1, at[i]].astype(f32) + more[b - 1, at[i]].astype(f32)
+
+        for b in range(len(bits) - 1):
+            for i in subs:
+                (firsts[i] if b == 0 else steps[b - 1][i]).wait()
+                summed[b, at[i]] = total(b, i).astype(bf16)
+                steps[b][i].start()
+        if meanwhile is not None:
+            meanwhile()
+        lasts = []
+        for i in subs:
+            (firsts[i] if len(bits) == 1 else steps[-1][i]).wait()
+            here = pl.ds(mine + i * size, size)
+            full[here] = total(len(bits) - 1, i).astype(bf16)
+            lasts.append(mp_copy(full.at[here], full.at[here], which, len(bits), i, 1))
+            lasts[i].start()
+            if ready is not None:
+                lasts[i].wait()
+                ready(i)
+        if ready is None:
+            for last in lasts:
+                last.wait()
 
     def exchange(which, src_at, dst, dst_at, size):
         def copy(k):
@@ -128,73 +149,80 @@
     def block(ref, size):
         return lambda i: ref.at[pl.ds(pl.multiple_of(i * size, size), size)]
 
+    def piece(ref, j, size):
+        return lambda i: ref.at[j, pl.ds(pl.multiple_of(i * size, size), size)]
+
+    def tiles(step):
+        def one(i, _):
+            step(pl.ds(pl.multiple_of(i * tile, tile), tile))
+            return 0
+
+        lax.fori_loop(0, triplets // tile, one, 0)
+
+    def in_part(at):
+        return one_hot(slot_total, in_ref[:, at])
+
+    def out_part(at):
+        return one_hot(slot_total, jnp.where(live_ref[:, at] > 0, out_ref[:, at], -1))
+
+    def angles(at):
+        angle[:, at] = lax.dot_general(
+            bw_ref[...], basis_ref[:, at], (((0,), (0,)), ((), ())),
+            precision=lax.Precision.HIGHEST, preferred_element_type=f32)
+
     part_a[...] = dot(state_ref[...], down_ref[...]).astype(bf16)
+    for i in range(graph):
+        lists_flat[:, i * cap:(i + 1) * cap] = lists_ref[0, i:i + 1, :]
+    list_hot[...] = one_hot(rows, lists_flat[...])
     pl.semaphore_wait(barrier, graph - 1 + len(bits))
-    mp_sum(0, part_a, got_a, sum_a, more_a, full_a)
+    mp_sum(0, part_a, got_a, sum_a, more_a, full_a, lambda: tiles(angles))
 
     step_rows = min(slot_total, 512)
     own = pl.ds(pl.multiple_of(g * cap, cap), cap)
 
     def pick(i, _):
         at = pl.ds(pl.multiple_of(i * step_rows, step_rows), step_rows)
-        lists = one_hot(rows, lists_ref[:, at])
-        to_a[at, :] = dot(lists, full_a[...], 0, 0).astype(bf16)
+        picked = dot(list_hot[:, at], full_a[...], 0, 0).astype(bf16)
+        for j in range(pieces):
+            to_a[j, at, :] = picked[:, j * lane:(j + 1) * lane]
         return 0
 
     lax.fori_loop(0, slot_total // step_rows, pick, 0)
-    start, wait = exchange(0, block(to_a, cap), from_a, block(from_a, cap), cap)
-    start()
-    from_a[own] = to_a[own]
-
-    def angles(i, _):
-        at = pl.ds(pl.multiple_of(i * tile, tile), tile)
-        angle[:, at] = lax.dot_general(
-            bw_ref[...], basis_ref[:, at], (((1,), (0,)), ((), ())),
-            precision=lax.Precision.HIGHEST, preferred_element_type=f32)
-        return 0
-
-    lax.fori_loop(0, triplets // tile, angles, 0)
-    slots[...] = jnp.zeros_like(slots)
-    wait()
-
-    recv_t[...] = from_a[...].astype(f32).T.astype(bf16)
-
-    def trips(i, _):
-        at = pl.ds(pl.multiple_of(i * tile, tile), tile)
-        source = one_hot(slot_total, in_ref[:, at])
-        value = dot(recv_t[...], source) * angle[:, at]
-        target = one_hot(slot_total, jnp.where(live_ref[:, at] > 0, out_ref[:, at], -1))
-        slots[...] += dot(target, value.astype(bf16), 1, 1)
-        return 0
-
-    lax.fori_loop(0, triplets // tile, trips, 0)
-    to_b[...] = slots[...].astype(bf16)
-
-    start, wait = exchange(1, block(to_b, cap), from_b, block(from_b, cap), cap)
-    start()
-    from_b[own] = to_b[own]
-    wait()
-
-    def put(i, total):
-        at = pl.ds(pl.multiple_of(i * step_rows, step_rows), step_rows)
-        return total + dot(one_hot(rows, lists_ref[:, at]), from_b[at, :])
-
-    if slot_total == step_rows:
-        part_b[...] = dot(one_hot(rows, lists_ref[...]), from_b[...]).astype(bf16)
-    else:
-        hidden[:, :trip] = jnp.zeros((rows, trip), f32)
-
-        def put(i, _):
-            at = pl.ds(pl.multiple_of(i * step_rows, step_rows), step_rows)
-            hidden[:, :trip] += dot(one_hot(rows, lists_ref[:, at]), from_b[at, :])
-            return 0
-
-        lax.fori_loop(0, slot_total // step_rows, put, 0)
-        part_b[...] = hidden[:, :trip].astype(bf16)
-    mp_sum(1, part_b, got_b, sum_b, more_b, full_b)
+    going = [exchange(j, piece(to_a, j, cap), from_a, piece(from_a, j, cap), cap) for j in range(pieces)]
+    back = [exchange(pieces + j, piece(to_b, j, cap), from_b, piece(from_b, j, cap), cap) for j in range(pieces)]
+    for start, _ in going:
+        start()
+    for j in range(pieces):
+        from_a[j, own] = to_a[j, own]
+    if kept:
+        def keep(at):
+            in_hot[:, at] = in_part(at)
+            out_hot[:, at] = out_part(at)
+
+        tiles(keep)
+
+    for j in range(pieces):
+        going[j][1]()
+        slots[...] = jnp.zeros_like(slots)
+        received = from_a[j].astype(f32).T.astype(bf16)
+
+        def trips(at):
+            source = in_hot[:, at] if kept else in_part(at)
+            value = dot(received, source) * angle[j * lane:(j + 1) * lane, at]
+            target = out_hot[:, at] if kept else out_part(at)
+            slots[...] += dot(target, value.astype(bf16), 1, 1)
+
+        tiles(trips)
+        to_b[j] = slots[...].astype(bf16)
+        back[j][0]()
+        from_b[j, own] = to_b[j, own]
+
+    for j in range(pieces):
+        back[j][1]()
+        part_b[:, j * lane:(j + 1) * lane] = dot(list_hot[...], from_b[j]).astype(bf16)
 
     plan, held = gather_plan(mp)
-    size = rows // CHUNKS
+    order = [h * len(subs) + i for i in subs for h in (0, 1)]
 
     def other_of(off):
         index = m
@@ -232,29 +260,31 @@
             if i not in relays_from:
                 act_copy(layer, c, i).wait_recv()
 
-    for c in range(CHUNKS):
-        at = pl.ds(c * size, size)
-        first = state_ref[at, :].astype(f32) + dot(full_b[at, :], up_ref[...])
-        hidden[at, :] = first
-        acts[0, m, at, :] = first.astype(bf16)
-        send(0, c)
-
+    def begin(i):
+        for c in order[2 * i:2 * i + 2]:
+            at = pl.ds(c * size, size)
+            first = state_ref[at, :].astype(f32) + dot(full_b[at, :], up_ref[...])
+            hidden[at, :] = first
+            acts[0, m, at, :] = first.astype(bf16)
+            send(0, c)
+
+    mp_sum(1, part_b, got_b, sum_b, more_b, full_b, ready=begin)
     load.wait()
-    relay(0, 0)
+    relay(0, order[0])
 
     def layer_step(l, _):
         for inside in range(2):
             k = 2 * l + inside
-            for c in range(CHUNKS):
+            for spot, c in enumerate(order):
                 at = pl.ds(c * size, size)
-                if c + 1 < CHUNKS:
-                    relay(k, c + 1)
+                if spot + 1 < CHUNKS:
+                    relay(k, order[spot + 1])
                 elif inside == 0:
-                    relay(k + 1, 0)
+                    relay(k + 1, order[0])
                 else:
                     @pl.when(l + 1 < layers)
                     def _():
-                        relay(k + 1, 0)
+                        relay(k + 1, order[0])
                 finish(k, c)
                 total = None
                 for off in held:
@@ -290,7 +320,7 @@
         return 0
 
     lax.fori_loop(0, atoms // atom_rows, collect, 0)
-    start, wait = exchange(2, block(atoms_to, ATOM_DEV), atoms_from, block(atoms_from, ATOM_DEV), ATOM_DEV)
+    start, wait = exchange(2 * pieces, block(atoms_to, ATOM_DEV), atoms_from, block(atoms_from, ATOM_DEV), ATOM_DEV)
     start()
     here = pl.ds(pl.multiple_of(g * ATOM_DEV, ATOM_DEV), ATOM_DEV)
     atoms_from[here] = jnp.zeros((ATOM_DEV, width), bf16)
@@ -303,7 +333,7 @@
     mine_out = silu(atom_scale * total).astype(bf16)
     table[here] = mine_out
     atom_out_ref[...] = mine_out
-    start, wait = exchange(3, lambda peer: block(table, ATOM_DEV)(g), table, block(table, ATOM_DEV), ATOM_DEV)
+    start, wait = exchange(2 * pieces + 1, lambda peer: block(table, ATOM_DEV)(g), table, block(table, ATOM_DEV), ATOM_DEV)
     start()
 
     def drain(k, _):
@@ -337,14 +367,21 @@
     extra = max(stages - 2, 1)
     half = rows // 2
     vmem = pltpu.VMEM
+    pieces = trip // 128 if trip % 128 == 0 else 1
+    hot_bytes = 2 * 2 * slot_total * triplets
+    hots = [vmem((slot_total, triplets), bf16)] * 2 if hot_bytes <= 2 ** 24 else [None, None]
     reduce_bufs = [
         vmem((rows, trip), bf16), vmem((half, trip), bf16), vmem((extra, half, trip), bf16),
         vmem((extra, half, trip), bf16), vmem((rows, trip), bf16),
     ]
     dma = pltpu.SemaphoreType.DMA
     spec = pl.BlockSpec(memory_space=pltpu.VMEM)
+    body = functools.partial(kernel, graph, mp, tile)
+    if hots[0] is None:
+        hots, kept_body, at = [], body, 37
+        body = lambda *refs: kept_body(*refs[:at], None, None, *refs[at:])
     return pl.pallas_call(
-        functools.partial(kernel, graph, mp, tile),
+        body,
         out_shape=(
             jax.ShapeDtypeStruct((rows, width), bf16),
             jax.ShapeDtypeStruct((ATOM_DEV, width), bf16),
@@ -354,25 +391,24 @@
         scratch_shapes=[
             vmem((maps,) + dense_weight.shape[2:], bf16), dma(()),
             *reduce_bufs, *reduce_bufs,
-            dma((2, stages)), dma((2, stages)),
-            vmem((slot_total, trip), bf16), vmem((slot_total, trip), bf16),
-            vmem((slot_total, trip), bf16), vmem((slot_total, trip), bf16),
-            dma((4, graph)), dma((4, graph)),
-            vmem((trip, slot_total), bf16), vmem((trip, triplets), f32), vmem((slot_total, trip), f32),
+            dma((2, stages, CHUNKS // 2)), dma((2, stages, CHUNKS // 2)),
+            *[vmem((pieces, slot_total, trip // pieces), bf16)] * 4,
+            dma((2 * pieces + 2, graph)), dma((2 * pieces + 2, graph)),
+            vmem((1, slot_total), jnp.int32), vmem((rows, slot_total), bf16),
+            vmem((trip, triplets), f32), vmem((slot_total, trip // pieces), f32), *hots,
             vmem((maps, mp, rows, width), bf16), vmem((rows, max(width, trip)), f32),
             dma((maps, CHUNKS, mp - 1)), dma((maps, CHUNKS, mp - 1)),
             vmem((atoms, width), f32), vmem((atoms, width), bf16), vmem((atoms, width), bf16),
             vmem((atoms, width), bf16),
-            vmem((8, 128), f32),
         ],
         compiler_params=pltpu.CompilerParams(
             collective_id=0, has_side_effects=True, vmem_limit_bytes=64000 * 1024
         ),
         name="edge_block",
     )(
-        edge_state, down_weight, basis, basis_weight.T, up_weight,
+        edge_state, down_weight, basis, basis_weight, up_weight,
         dense_weight.reshape((maps,) + dense_weight.shape[2:]),
-        send_rows.reshape(1, slot_total), trip_in.reshape(1, triplets), trip_out.reshape(1, triplets),
+        send_rows, trip_in.reshape(1, triplets), trip_out.reshape(1, triplets),
         trip_live.reshape(1, triplets), edge_atom.reshape(1, rows),
     )
 

time: 130 us -> 122 us (0.938)
  Pallas kernels: 123 us -> 118 us
  local copies, waits for them, and re-layouts: 6.16 us -> 3.13 us
    pallas_call x1, Pallas kernels: 123 us -> 118 us  [local(): pl.pallas_call(body, out_shape=(jax.ShapeDtypeStruct((rows, width), bf16)...]
    unnamed x3 -> x2, local copies, waits for them, and re-layouts: 4.82 us -> 3.13 us
    reshape x1 -> x0, local copies, waits for them, and re-layouts: 1.34 us -> none  [local(): send_rows.reshape(1, slot_total)]
where the time goes in v2:
time: 122 us
  Pallas kernels  118 us (97%)
  local copies, waits for them, and re-layouts  3.13 us (3%)
    pallas_call x1, Pallas kernels, local(): pl.pallas_call(body, out_shape=(jax.ShapeDtypeStruct((rows, width), bf16)...  118 us
    unnamed x2, local copies, waits for them, and re-layouts  3.13 us

profile of v2, /device:TPU:0, one launch (start us, length us, event | category | flops | bytes accessed | tf_op | source)
XLA Modules:
  0.0 122.1 jit_solution(4854851314058368763)
XLA Ops:
  0.6 118.4 %edge_block.1 = (bf16[512,384]{1,0:T(8,128)(2,1)}, bf16[32,384]{1,0:T(8,128)(2,1)}) custom-call(bf16[512,384]{1,0:T(8,128)(2,1)} %state_ref.1, bf16[384,384]{1,0:T(8,128)(2,1)} %down_ref.1, f32[42,4096]{1,0:T(8,128)} %basis_ref.1, f32[42,384]{1,0:T(8,128)} %bw_ref.1, bf16[384,384]{1,0:T(8,128)(2,1)} %up_ref.1, bf16[6,1536,384]{2,1,0:T(8,128)(2,1)} %bitcast.5, ...), custom_call_target="tpu_custom_call" | custom-call | tf_op jit(solution)/shard_map/edge_block/pallas_call | solution.py:383
  119.0 1.8 %copy.15 = bf16[512,384]{1,0:T(8,128)(2,1)} copy(bf16[512,384]{1,0:T(8,128)(2,1)} %get-tuple-element.4) | data formatting | bytes 786432
  120.8 1.3 %copy.16 = bf16[32,384]{1,0:T(8,128)(2,1)} copy(bf16[32,384]{1,0:T(8,128)(2,1)} %get-tuple-element.5) | data formatting | bytes 49152

commit v3 on v2

--- a/solution.py
+++ b/solution.py
@@ -354,6 +354,11 @@
     edge_out_ref[...] = hidden[...].astype(bf16)
 
 
+def hand_on(edge_ref, atom_ref, edge_out_ref, atom_out_ref):
+    edge_out_ref[...] = edge_ref[...]
+    atom_out_ref[...] = atom_ref[...]
+
+
 def local(graph, mp, edge_state, down_weight, basis, basis_weight, up_weight, dense_weight,
           send_rows, trip_in, trip_out, trip_live, edge_atom):
     rows, width = edge_state.shape
@@ -361,7 +366,7 @@
     slot_total = graph * send_rows.shape[2]
     triplets = trip_in.shape[0]
     maps = dense_weight.shape[0] * dense_weight.shape[1]
-    tile = 512 if slot_total <= 512 else 128
+    tile = 2048 if slot_total <= 512 else 128
     atoms = graph * ATOM_DEV
     stages = mp.bit_length()
     extra = max(stages - 2, 1)
@@ -380,7 +385,7 @@
     if hots[0] is None:
         hots, kept_body, at = [], body, 37
         body = lambda *refs: kept_body(*refs[:at], None, None, *refs[at:])
-    return pl.pallas_call(
+    outs = pl.pallas_call(
         body,
         out_shape=(
             jax.ShapeDtypeStruct((rows, width), bf16),
@@ -411,6 +416,13 @@
         send_rows, trip_in.reshape(1, triplets), trip_out.reshape(1, triplets),
         trip_live.reshape(1, triplets), edge_atom.reshape(1, rows),
     )
+    return pl.pallas_call(
+        hand_on,
+        out_shape=tuple(jax.ShapeDtypeStruct(o.shape, o.dtype) for o in outs),
+        in_specs=[spec] * 2,
+        out_specs=(spec, spec),
+        name="hand_on",
+    )(*outs)
 
 
 def solution(mesh):

time: 122 us -> 116 us (0.951)
  local copies, waits for them, and re-layouts: 3.13 us -> 0 us
  Pallas kernels: 118 us -> 115 us
    pallas_call x1, Pallas kernels: 118 us -> 114 us  [local(): pl.pallas_call(body, out_shape=(jax.ShapeDtypeStruct((rows, width), bf16)...]
    unnamed x2 -> x0, local copies, waits for them, and re-layouts: 3.13 us -> none
    pallas_call x0 -> x1, Pallas kernels: none -> 1.78 us  [local(): pl.pallas_call(hand_on, out_shape=tuple((jax.ShapeDtypeStruct(o.shape, o....]
where the time goes in v3:
time: 116 us
  Pallas kernels  115 us (99%)
    pallas_call x1, Pallas kernels, local(): pl.pallas_call(body, out_shape=(jax.ShapeDtypeStruct((rows, width), bf16)...  114 us

profile of v3, /device:TPU:0, one launch (start us, length us, event | category | flops | bytes accessed | tf_op | source)
XLA Modules:
  0.0 116.1 jit_solution(4743877682821652171)
XLA Ops:
  0.6 113.7 %edge_block.1 = (bf16[512,384]{1,0:T(8,128)(2,1)}, bf16[32,384]{1,0:T(8,128)(2,1)}) custom-call(bf16[512,384]{1,0:T(8,128)(2,1)} %state_ref.1, bf16[384,384]{1,0:T(8,128)(2,1)} %down_ref.1, f32[42,4096]{1,0:T(8,128)} %basis_ref.1, f32[42,384]{1,0:T(8,128)} %bw_ref.1, bf16[384,384]{1,0:T(8,128)(2,1)} %up_ref.1, bf16[6,1536,384]{2,1,0:T(8,128)(2,1)} %bitcast.5, ...), custom_call_target="tpu_custom_call" | custom-call | tf_op jit(solution)/shard_map/edge_block/pallas_call | solution.py:388
  114.3 1.8 %hand_on.1 = (bf16[512,384]{1,0:T(8,128)(2,1)}, bf16[32,384]{1,0:T(8,128)(2,1)}) custom-call(bf16[512,384]{1,0:T(8,128)(2,1)} %get-tuple-element.4.edge_ref, bf16[32,384]{1,0:T(8,128)(2,1)} %get-tuple-element.5.atom_ref), custom_call_target="tpu_custom_call" | custom-call | tf_op jit(solution)/shard_map/hand_on/pallas_call | solution.py:419
